TPU v7x, 32 devices: a whole 2x2x4 slice. The times are simulated.
32 devices in a mesh: group: 2 (over x), lat: 16 (over z, y, core).
Axes of the slice: x: 2, y: 2, z: 4, core: 2. Of those that a mesh axis runs over, the one named last changes fastest.
Arguments:
- grid_values: bfloat16 [224, 1440, 256], P(('group', 'lat')), parts along dimension 0, may hold values from -630 to 630
- lat_counts: int32 [16], replicated, may hold values from 1 to 7, 96 in all
- owner_wavenumber: int32 [384], replicated, may hold values from 0 to 383, each once
- legendre: bfloat16 [384, 96, 384], P('lat'), may hold values from -0.625 to 0.625
- quad_weight: float32 [96], replicated, may hold values from 0.3 to 3
- spectral_gain: float32 [384, 256], replicated, may hold values from 0.3 to 3
- channel_mix: bfloat16 [256, 256], replicated, may hold values from -0.375 to 0.375
Outputs:
- grid_output: bfloat16 [224, 1440, 256], P(('group', 'lat')), parts along dimension 0
There are 2 independent parts, one for each index of `group`. A program takes and returns all parts, laid end to end along the dimension named above; an argument that names none is the same for every part. Nothing has to cross between parts.
Inputs may be any that keep to these rules, and one draw needn't show every extreme that they name: `lat_counts`: some device has all 7 slots live. `owner_wavenumber`: each wavenumber appears once; device i of lat owns wavenumber slots i * 24 to (i + 1) * 24 - 1.
All inputs are finite; a program needn't handle non-finite values.
Results may differ from a plain program's by a relative error of at most 0.0095.
Values may be sent and summed in bfloat16 or wider, within the bound.
A program may use at most 64 MiB of HBM per device.

v0:
```python
import math

import jax
import jax.numpy as jnp
from jax import lax
from jax.sharding import PartitionSpec as P


def live_slots(lat_counts, slot_count, live_total):
    devices = lat_counts.shape[0]
    starts = jnp.cumsum(lat_counts) - lat_counts
    device_ids = jnp.arange(devices, dtype=jnp.int32)
    slot_ids = jnp.arange(devices * slot_count, dtype=jnp.int32)
    holder = slot_ids // slot_count
    within = slot_ids - holder * slot_count
    holder_hot = holder[:, None] == device_ids[None, :]
    holder_count = jnp.sum(jnp.where(holder_hot, lat_counts[None, :], 0), axis=1)
    holder_start = jnp.sum(jnp.where(holder_hot, starts[None, :], 0), axis=1)
    slot_valid = within < holder_count
    slot_live = jnp.where(slot_valid, holder_start + within, 0)
    live_ids = jnp.arange(live_total, dtype=jnp.int32)
    reached = (starts[None, :] <= live_ids[:, None]).astype(jnp.int32)
    source = jnp.sum(reached, axis=1) - 1
    source_hot = source[:, None] == device_ids[None, :]
    source_start = jnp.sum(jnp.where(source_hot, starts[None, :], 0), axis=1)
    live_slot = source * slot_count + live_ids - source_start
    return (slot_valid, slot_live, live_slot)


def wave_angles(wave_list, longitudes):
    points = jnp.arange(longitudes, dtype=jnp.int32)
    phase = wave_list[:, None] * points[None, :] % longitudes
    return phase.astype(jnp.float32) * (2.0 * math.pi / longitudes)


def forward_table(wave_list, longitudes):
    angle = wave_angles(wave_list, longitudes)
    factor = 1.0 / math.sqrt(longitudes)
    return jnp.stack([jnp.cos(angle) * factor, -jnp.sin(angle) * factor], axis=1).astype(
        jnp.bfloat16
    )


def inverse_table(wave_list, longitudes):
    angle = wave_angles(wave_list, longitudes)
    factor = 1.0 / math.sqrt(longitudes)
    doubled = jnp.where(wave_list > 0, 2.0, 1.0).astype(jnp.float32)[:, None] * factor
    return jnp.stack([jnp.cos(angle) * doubled, -jnp.sin(angle) * doubled], axis=1).astype(
        jnp.bfloat16
    )


def body(
    grid_values, lat_counts, owner_wavenumber, legendre, quad_weight, spectral_gain, channel_mix
):
    slot_count, longitudes, channels = grid_values.shape
    my_index = lax.axis_index("lat")
    wave_count = owner_wavenumber.shape[0]
    wave_share, live_total, degrees = legendre.shape
    slot_valid, slot_live, live_slot = live_slots(lat_counts, slot_count, live_total)
    local_valid = lax.dynamic_slice_in_dim(slot_valid, my_index * slot_count, slot_count)
    row_weight = local_valid.astype(jnp.float32)[:, None, None]
    widened = grid_values.astype(jnp.float32) * row_weight
    totals = lax.psum(
        (jnp.sum(widened, axis=(0, 1)), jnp.sum(widened * widened, axis=(0, 1))), "lat"
    )
    points = live_total * longitudes
    channel_mean = totals[0] / points
    variance = totals[1] / points - channel_mean * channel_mean
    normed = (
        (grid_values.astype(jnp.float32) - channel_mean) * lax.rsqrt(variance + 1e-05) * row_weight
    ).astype(jnp.bfloat16)
    forward_flat = forward_table(owner_wavenumber, longitudes).reshape(2 * wave_count, longitudes)
    spectra = jnp.einsum("skc,qk->sqc", normed, forward_flat, preferred_element_type=jnp.float32)
    spectra = spectra.astype(jnp.bfloat16).reshape(slot_count, wave_count, 2, normed.shape[2])
    received = lax.all_to_all(spectra, "lat", split_axis=1, concat_axis=0, tiled=True)
    own_waves = lax.dynamic_slice_in_dim(owner_wavenumber, my_index * wave_share, wave_share)
    degree_mask = (jnp.arange(degrees, dtype=jnp.int32)[None, :] >= own_waves[:, None]).astype(
        jnp.float32
    )
    gathered = jnp.take(received, live_slot, axis=0)
    weighted = (gathered.astype(jnp.float32) * quad_weight[:, None, None, None]).astype(
        jnp.bfloat16
    )
    coefficient = jnp.einsum(
        "rgl,grtc->rltc", legendre, weighted, preferred_element_type=jnp.float32
    )
    filtered = (
        coefficient * degree_mask[:, :, None, None] * spectral_gain[None, :, None, :]
    ).astype(jnp.bfloat16)
    mixed = jnp.dot(filtered.reshape(-1, channels), channel_mix, preferred_element_type=jnp.float32)
    mixed = mixed.astype(jnp.bfloat16).reshape(wave_share, degrees, 2, channels)
    synthesis = jnp.einsum(
        "rgl,rltc->grtc", legendre, mixed, preferred_element_type=jnp.float32
    ).astype(jnp.bfloat16)
    outgoing = jnp.where(
        slot_valid[:, None, None, None],
        jnp.take(synthesis, slot_live, axis=0),
        jnp.zeros((), jnp.bfloat16),
    )
    inverse_flat = inverse_table(owner_wavenumber, longitudes).reshape(2 * wave_count, longitudes)
    returned = lax.all_to_all(outgoing, "lat", split_axis=0, concat_axis=1, tiled=True)
    flat_back = returned.reshape(slot_count, 2 * wave_count, returned.shape[3])
    return jnp.einsum(
        "sqc,qk->skc", flat_back, inverse_flat, preferred_element_type=jnp.float32
    ).astype(jnp.bfloat16)


def solution(mesh):
    return jax.shard_map(
        body,
        mesh=mesh,
        in_specs=(P(("group", "lat"), None, None), P(), P(), P("lat", None, None), P(), P(), P()),
        out_specs=P(("group", "lat"), None, None),
        check_vma=False,
    )
```

profile of v0, /device:TPU:13, one launch (start us, length us, event | category | flops | bytes accessed | tf_op | source)
XLA Modules:
  0.0 337.3 jit_solution(7146616504685830470)
XLA Ops:
  2.4 10.7 %multiply_convert_fusion.4 = (bf16[384,1,1440]{0,2,1:T(8,128)(2,1)S(1)}, bf16[384,1,1440]{0,2,1:T(8,128)(2,1)S(1)}, bf16[384,1,1440]{0,2,1:T(8,128)(2,1)S(1)}, bf16[384,1,1440]{0,2,1:T(8,128)(2,1)S(1)}) fusion(f32[384]{0:T(512)S(1)} %select_multiply_fusion, s32[384]{0:T(512)} %param.9), kind=kLoop, calls=%fused_computation.36 | loop fusion | flops 9953280 | bytes 4426752 | tf_op jit(solution)/shard_map/convert.2
  15.6 6.8 %copy.58 = bf16[384,2,1440]{2,1,0:T(2,128)(2,1)} copy(bf16[384,2,1440]{0,2,1:T(8,128)(2,1)} %get-tuple-element.20) | data formatting | bytes 4423680 | tf_op jit(solution)/shard_map/stack | solution.py:39
  22.4 6.0 %convert_element_type.92 = bf16[768,1440]{1,0:T(8,128)(2,1)} reshape(bf16[384,2,1440]{2,1,0:T(2,128)(2,1)} %copy.58) | data formatting | bytes 4423680 | tf_op jit(solution)/shard_map/convert_element_type | solution.py:39
  28.6 4.8 %fusion.2 = (f32[256]{0:T(256)S(1)}, f32[256]{0:T(256)S(1)}) fusion(bf16[7,1440,256]{2,1,0:T(8,128)(2,1)} %param.7, f32[7]{0:T(128)S(1)} %dynamic-slice_convert_fusion), kind=kLoop, calls=%fused_computation.8 | loop fusion | flops 12901888 | bytes 5163036 | tf_op jit(solution)/shard_map/reduce_sum | solution.py:65
  33.4 21.9 %all-reduce = (f32[256]{0:T(256)S(1)}, f32[256]{0:T(256)S(1)}) all-reduce(f32[256]{0:T(256)S(1)} %get-tuple-element.6, f32[256]{0:T(256)S(1)} %get-tuple-element.5), channel_id=1, replica_groups=mesh['group'=2,'lat'=16] {'lat'}, use_global_device_ids=true, to_apply=%region_8.9 | all-reduce | flops 512 | bytes 4096 | tf_op jit(solution)/shard_map/psum | solution.py:64
  55.4 9.3 %convert_bitcast_fusion.1 = bf16[7,768,256]{2,1,0:T(8,128)(2,1)} fusion(bf16[7,1440,256]{2,1,0:T(8,128)(2,1)} %param.7, f32[256]{0:T(256)S(1)} %get-tuple-element.16, f32[256]{0:T(256)S(1)} %get-tuple-element.15, f32[7]{0:T(128)S(1)} %dynamic-slice_convert_fusion, bf16[768,1440]{1,0:T(8,128)(2,1)} %convert_element_type.92), kind=kOutput, calls=%fused_computation.23 | convolution fusion | flops 3977895936 | bytes 10127388 | tf_op jit(solution)/shard_map/skc,qk->sqc/dot_general | solution.py:74
  64.6 6.5 %reshape.389 = bf16[7,384,2,256]{3,2,1,0:T(2,128)(2,1)} reshape(bf16[7,768,256]{2,1,0:T(8,128)(2,1)} %convert_bitcast_fusion.1) | data formatting | bytes 5505024 | tf_op jit(solution)/shard_map/reshape | solution.py:75
  71.1 5.2 %copy.60 = bf16[7,384,2,256]{3,2,0,1:T(2,128)(2,1)} copy(bf16[7,384,2,256]{3,2,1,0:T(2,128)(2,1)} %reshape.389) | data formatting | bytes 5505024 | tf_op jit(solution)/shard_map/reshape | solution.py:75
  76.3 16.8 %all-to-all-start = ((bf16[7,384,2,256]{3,2,0,1:T(2,128)(2,1)}), bf16[7,384,2,256]{3,2,0,1:T(2,128)(2,1)}, u32[]{:S(2)}, u32[]{:S(2)}) async-start(bf16[7,384,2,256]{3,2,0,1:T(2,128)(2,1)} %copy.60), calls=%async_computation | async-start | bytes 5505024 | tf_op jit(solution)/shard_map/all_to_all | solution.py:76
  94.4 60.3 %all-to-all-done = bf16[7,384,2,256]{3,2,0,1:T(2,128)(2,1)} async-done(((bf16[7,384,2,256]{3,2,0,1:T(2,128)(2,1)}), bf16[7,384,2,256]{3,2,0,1:T(2,128)(2,1)}, u32[]{:S(2)}, u32[]{:S(2)}) %all-to-all-start) | async-done | bytes 2752544 | tf_op jit(solution)/shard_map/all_to_all | solution.py:76
  158.6 4.0 %gather_fusion = bf16[96,24,2,256]{3,1,2,0:T(8,128)(2,1)} fusion(bf16[112,24,2,256]{3,1,2,0:T(8,128)(2,1)} %bitcast.59, s32[1024]{0:T(1024)S(1)} %pad_clamp_fusion.1), kind=kCustom, calls=%fused_computation | custom fusion | bytes 4718976 | tf_op jit(solution)/shard_map/jit(_take)/gather | solution.py:81
  165.0 6.1 %fusion = bf16[24,384,2,256]{1,3,2,0:T(8,128)(2,1)} fusion(f32[384,256]{0,1:T(8,128)S(1)} %copy.64, f32[24,384]{1,0:T(8,128)S(1)} %fusion.31, bf16[96,24,2,256]{3,1,2,0:T(8,128)(2,1)S(1)} %multiply_convert_fusion, bf16[24,96,384]{2,1,0:T(8,128)(2,1)S(1)} %copy-done), kind=kOutput, calls=%fused_computation.4 | convolution fusion | flops 920125440 | bytes 13996032 | tf_op jit(solution)/shard_map/rgl,grtc->rltc/dot_general | solution.py:85
  171.1 23.6 %copy.65 = bf16[24,384,2,256]{3,2,1,0:T(2,128)(2,1)} copy(bf16[24,384,2,256]{1,3,2,0:T(8,128)(2,1)} %fusion) | data formatting | bytes 18874368 | tf_op jit(solution)/shard_map/convert_element_type | solution.py:90
  194.7 14.6 %reshape.390 = bf16[18432,256]{1,0:T(8,128)(2,1)} reshape(bf16[24,384,2,256]{3,2,1,0:T(2,128)(2,1)} %copy.65) | data formatting | bytes 18874368 | tf_op jit(solution)/shard_map/reshape | solution.py:91
  209.3 9.9 %convolution_convert_fusion = bf16[18432,256]{1,0:T(8,128)(2,1)} fusion(bf16[18432,256]{1,0:T(8,128)(2,1)} %reshape.390, bf16[256,256]{1,0:T(8,128)(2,1)S(1)} %copy-done.2), kind=kOutput, calls=%fused_computation.2 | convolution fusion | flops 2420637696 | bytes 19005440 | tf_op jit(solution)/shard_map/dot_general | solution.py:91
  219.2 14.6 %reshape.391 = bf16[24,384,2,256]{3,2,1,0:T(2,128)(2,1)} reshape(bf16[18432,256]{1,0:T(8,128)(2,1)} %convolution_convert_fusion) | data formatting | bytes 18874368 | tf_op jit(solution)/shard_map/reshape | solution.py:92
  233.8 5.6 %convert_bitcast_fusion.2 = bf16[96,24,2,256]{3,0,2,1:T(8,128)(2,1)S(1)} fusion(bf16[24,384,2,256]{3,2,1,0:T(2,128)(2,1)} %reshape.391, bf16[24,96,384]{2,1,0:T(8,128)(2,1)S(1)} %copy-done), kind=kOutput, calls=%fused_computation.27 | convolution fusion | flops 907149312 | bytes 13565952 | tf_op jit(solution)/shard_map/rgl,rltc->grtc/dot_general | solution.py:93
  249.4 4.8 %all-to-all-start.1 = ((bf16[112,24,2,256]{3,1,2,0:T(8,128)(2,1)}), bf16[112,24,2,256]{3,1,2,0:T(8,128)(2,1)}, u32[]{:S(2)}, u32[]{:S(2)}) async-start(bf16[112,24,2,256]{3,1,2,0:T(8,128)(2,1)} %select_select_fusion), calls=%async_computation.1 | async-start | bytes 5505024 | tf_op jit(solution)/shard_map/all_to_all | solution.py:102
  254.2 6.9 %copy.56 = bf16[384,2,1440]{2,1,0:T(2,128)(2,1)} copy(bf16[384,2,1440]{0,2,1:T(8,128)(2,1)} %get-tuple-element.19) | data formatting | bytes 4423680 | tf_op jit(solution)/shard_map/stack | solution.py:48
  261.0 6.0 %convert_element_type.90 = bf16[768,1440]{1,0:T(8,128)(2,1)} reshape(bf16[384,2,1440]{2,1,0:T(2,128)(2,1)} %copy.56) | data formatting | bytes 4423680 | tf_op jit(solution)/shard_map/convert_element_type | solution.py:48
  267.1 48.7 %all-to-all-done.1 = bf16[112,24,2,256]{3,1,2,0:T(8,128)(2,1)} async-done(((bf16[112,24,2,256]{3,1,2,0:T(8,128)(2,1)}), bf16[112,24,2,256]{3,1,2,0:T(8,128)(2,1)}, u32[]{:S(2)}, u32[]{:S(2)}) %all-to-all-start.1) | async-done | bytes 2752544 | tf_op jit(solution)/shard_map/all_to_all | solution.py:102
  315.7 5.8 %copy.68 = bf16[7,16,24,2,256]{4,3,2,1,0:T(2,128)(2,1)} copy(bf16[7,16,24,2,256]{4,2,3,0,1:T(8,128)(2,1)} %bitcast.18) | data formatting | bytes 5505024 | tf_op jit(solution)/shard_map/all_to_all | solution.py:102
  321.5 6.8 %reshape.392 = bf16[7,768,256]{2,1,0:T(8,128)(2,1)} reshape(bf16[7,16,24,2,256]{4,3,2,1,0:T(2,128)(2,1)} %copy.68) | data formatting | bytes 5505024 | tf_op jit(solution)/shard_map/reshape | solution.py:103
  328.3 9.0 %convert_bitcast_fusion = bf16[7,1440,256]{2,1,0:T(8,128)(2,1)} fusion(bf16[7,768,256]{2,1,0:T(8,128)(2,1)} %reshape.392, bf16[768,1440]{1,0:T(8,128)(2,1)} %convert_element_type.90), kind=kOutput, calls=%fused_computation.16 | convolution fusion | flops 3966197760 | bytes 10125312 | tf_op jit(solution)/shard_map/sqc,qk->skc/dot_general | solution.py:104
  (38 shorter events, 22.6 us)
Async XLA Ops:
  0.0 165.0 %copy-start = (bf16[24,96,384]{2,1,0:T(8,128)(2,1)S(1)}, bf16[24,96,384]{2,1,0:T(8,128)(2,1)}, u32[]{:S(2)}) copy-start(bf16[24,96,384]{2,1,0:T(8,128)(2,1)} %param.10) | copy-start | bytes 5308420
  22.4 6.0 %copy-start.3 = (s32[16]{0:T(128)S(1)}, s32[16]{0:T(128)}, u32[]{:S(2)}) copy-start(s32[16]{0:T(128)} %param.8) | copy-start | bytes 196
  76.3 17.5 %copy-start.1 = (f32[384,256]{1,0:T(8,128)S(1)}, f32[384,256]{1,0:T(8,128)}, u32[]{:S(2)}) copy-start(f32[384,256]{1,0:T(8,128)} %param.12) | copy-start | bytes 1179652
  76.3 78.3 %all-to-all-start = ((bf16[7,384,2,256]{3,2,0,1:T(2,128)(2,1)}), bf16[7,384,2,256]{3,2,0,1:T(2,128)(2,1)}, u32[]{:S(2)}, u32[]{:S(2)}) async-start(bf16[7,384,2,256]{3,2,0,1:T(2,128)(2,1)} %copy.60), calls=%async_computation | async-start | bytes 5505024 | tf_op jit(solution)/shard_map/all_to_all | solution.py:76
  158.6 4.0 %copy-start.4 = (f32[96]{0:T(128)S(1)}, f32[96]{0:T(128)}, u32[]{:S(2)}) copy-start(f32[96]{0:T(128)} %param.11) | copy-start | bytes 1156
  194.7 14.6 %copy-start.2 = (bf16[256,256]{1,0:T(8,128)(2,1)S(1)}, bf16[256,256]{1,0:T(8,128)(2,1)}, u32[]{:S(2)}) copy-start(bf16[256,256]{1,0:T(8,128)(2,1)} %param.13) | copy-start | bytes 393220
  249.4 66.3 %all-to-all-start.1 = ((bf16[112,24,2,256]{3,1,2,0:T(8,128)(2,1)}), bf16[112,24,2,256]{3,1,2,0:T(8,128)(2,1)}, u32[]{:S(2)}, u32[]{:S(2)}) async-start(bf16[112,24,2,256]{3,1,2,0:T(8,128)(2,1)} %select_select_fusion), calls=%async_computation.1 | async-start | bytes 5505024 | tf_op jit(solution)/shard_map/all_to_all | solution.py:102
where the time goes:
time: 340 us; the launch traced here: 337 us
  local copies, waits for them, and re-layouts  119 us (35%)
  waiting for transfers between devices  109 us (32%)
  matrix products  39.9 us (12%)
  other arithmetic  25.5 us (8%)
  blocking collectives  21.9 us (6%)
  starting transfers between devices  21.5 us (6%)
    all_to_all x1, waiting for transfers between devices, body(): lax.all_to_all(spectra, 'lat', split_axis=1, concat_axis=0, tiled=True)  60.3 us
    all_to_all x1, waiting for transfers between devices, body(): lax.all_to_all(outgoing, 'lat', split_axis=0, concat_axis=1, tiled=True)  48.7 us
    convert_element_type x1, local copies, waits for them, and re-layouts, body(): filtered = (coefficient * degree_mask[:, :, None, None] * spectral_gain[N...  23.6 us
    psum x1, blocking collectives, body(): lax.psum((jnp.sum(widened, axis=(0, 1)), jnp.sum(widened * widened, axis=...  21.9 us
    all_to_all x1, starting transfers between devices, body(): lax.all_to_all(spectra, 'lat', split_axis=1, concat_axis=0, tiled=True)  16.8 us
    reshape x1, local copies, waits for them, and re-layouts, body(): filtered.reshape(-1, channels)  14.6 us
    reshape x1, local copies, waits for them, and re-layouts, body(): mixed = mixed.astype(jnp.bfloat16).reshape(wave_share, degrees, 2, channels)  14.6 us
    reshape x2, local copies, waits for them, and re-layouts, body(): spectra.astype(jnp.bfloat16)  11.7 us
  transfers between devices with their start and end apart: 2, of which 2 were waited for; matrix products, arithmetic and copies ran while one was open for 4% of the time, Pallas kernels for 0%

commit v1 on v0

v1 whole, which is shorter than its diff:
```python
import functools
import math

import jax
import jax.numpy as jnp
import numpy as np
from jax import lax
from jax.experimental import pallas as pl
from jax.experimental.pallas import tpu as pltpu
from jax.sharding import PartitionSpec as P

BLOCK = 8
F32 = jnp.float32
BF16 = jnp.bfloat16


def trig_table(waves, longitudes):
    phase = np.arange(waves)[:, None] * np.arange(longitudes)[None, :] % longitudes
    angle = phase * (2.0 * math.pi / longitudes)
    factor = 1.0 / math.sqrt(longitudes)
    table = np.concatenate([np.cos(angle) * factor, -np.sin(angle) * factor], axis=0)
    return table.astype(BF16)


def greet_all(axis, count, me):
    barrier = pltpu.get_barrier_semaphore()

    def signal(i, carry):
        other = lax.rem(me + i, count)
        pl.semaphore_signal(
            barrier, inc=1, device_id={axis: other}, device_id_type=pl.DeviceIdType.MESH
        )
        return carry

    lax.fori_loop(1, count, signal, 0)
    return barrier


def forward_kernel(
    axis, n, points, counts, x, base, rows, recv, back_table,
    sums, table, normed, spec, mom_send, mom_recv, send, arrive, own,
):
    me = lax.axis_index(axis)
    slots = x.shape[0]
    barrier = greet_all(axis, n, me)
    live = counts[me]
    zero = jnp.zeros((1, x.shape[2]), F32)

    def add_slot(s, carry):
        first, second = carry
        wide = x[s].astype(F32)
        weight = jnp.where(s < live, 1.0, 0.0).astype(F32)
        first = first + weight * jnp.sum(wide, axis=0, keepdims=True)
        second = second + weight * jnp.sum(wide * wide, axis=0, keepdims=True)
        return first, second

    first, second = lax.fori_loop(0, slots, add_slot, (zero, zero))
    sums[me, 0:1, :] = first
    sums[me, 1:2, :] = second
    pl.semaphore_wait(barrier, n - 1)

    def moment_copy(i):
        other = lax.rem(me + i, n)
        return pltpu.make_async_remote_copy(
            src_ref=sums.at[me], dst_ref=sums.at[me],
            send_sem=mom_send.at[i], recv_sem=mom_recv.at[i],
            device_id={axis: other}, device_id_type=pl.DeviceIdType.MESH,
        )

    def start_moment(i, carry):
        moment_copy(i).start()
        return carry

    def wait_moment(i, carry):
        moment_copy(i).wait()
        return carry

    lax.fori_loop(1, n, start_moment, 0)
    total = base.shape[0]
    chosen = rows[...] == lax.broadcasted_iota(jnp.int32, (rows.shape[0], total), 1)
    chosen = jnp.where(chosen, 1.0, 0.0).astype(BF16)
    table[...] = jnp.dot(chosen, base[...], preferred_element_type=F32).astype(BF16)
    lax.fori_loop(1, n, wait_moment, 0)
    both = jnp.sum(sums[...], axis=0)
    mean = both[0:1] / points
    variance = both[1:2] / points - mean * mean
    scale = lax.rsqrt(variance + 1e-05)

    def block_copy(i, s):
        other = lax.rem(me + i, n)
        return pltpu.make_async_remote_copy(
            src_ref=spec.at[other, s], dst_ref=recv.at[me, s],
            send_sem=send.at[i], recv_sem=arrive.at[i],
            device_id={axis: other}, device_id_type=pl.DeviceIdType.MESH,
        )

    def slot_step(s, carry):
        weight = jnp.where(s < live, 1.0, 0.0).astype(F32)
        normed[...] = ((x[s].astype(F32) - mean) * scale * weight).astype(BF16)
        out = jnp.dot(table[...], normed[...], preferred_element_type=F32).astype(BF16)
        spec[:, s] = out.reshape(spec.shape[0], spec.shape[2], spec.shape[3])

        def start_block(i, inner):
            block_copy(i, s).start()
            return inner

        lax.fori_loop(1, n, start_block, 0)
        return carry

    lax.fori_loop(0, slots, slot_step, 0)
    mine = pltpu.make_async_copy(spec.at[me], recv.at[me], own)
    mine.start()
    back_table[...] = table[...].T

    def wait_block(i, carry):
        other = lax.rem(me + i, n)
        pltpu.make_async_remote_copy(
            src_ref=spec.at[other], dst_ref=recv.at[me],
            send_sem=send.at[i], recv_sem=arrive.at[i],
            device_id={axis: other}, device_id_type=pl.DeviceIdType.MESH,
        ).wait()
        return carry

    lax.fori_loop(1, n, wait_block, 0)
    mine.wait()


def middle_kernel(
    axis, n, share, counts, owner, spectra, legendre, quad, gain, mix, back,
    gathered, pick, quad_slot, outgoing, result, send, arrive, own,
):
    me = lax.axis_index(axis)
    slots, height = spectra.shape[1], spectra.shape[2]
    everything = n * slots
    live_total, degrees = legendre.shape[1], legendre.shape[2]
    channels = mix.shape[0]
    halves = channels // 128
    blocks = height // (2 * BLOCK)
    barrier = greet_all(axis, n, me)

    row = lax.broadcasted_iota(jnp.int32, (everything, live_total), 0)
    lane = lax.broadcasted_iota(jnp.int32, (everything, live_total), 1)
    pick[...] = jnp.zeros_like(pick)

    def mark(i, begin):
        within = row - i * slots
        hit = (within >= 0) & (within < counts[i]) & (lane == begin + within)
        pick[...] += jnp.where(hit, 1.0, 0.0).astype(F32)
        return begin + counts[i]

    lax.fori_loop(0, n, mark, jnp.int32(0))
    quad_slot[...] = jnp.broadcast_to(
        jnp.sum(pick[...] * quad[...], axis=1, keepdims=True), quad_slot.shape
    )

    def widen(i, carry):
        for s in range(slots):
            wide = spectra[i, s].astype(F32)
            begin = pl.multiple_of((i * slots + s) * height, 8)
            for h in range(halves):
                gathered[h, pl.ds(begin, height), :] = wide[:, h * 128 : (h + 1) * 128]
        return carry

    lax.fori_loop(0, n, widen, 0)
    degree = lax.broadcasted_iota(jnp.int32, (degrees, channels), 0)

    def block_copy(i, b):
        other = lax.rem(me + i, n)
        return pltpu.make_async_remote_copy(
            src_ref=outgoing.at[b, other],
            dst_ref=back.at[me, :, pl.ds(b * 2 * BLOCK, 2 * BLOCK), :],
            send_sem=send.at[b, i], recv_sem=arrive.at[b, i],
            device_id={axis: other}, device_id_type=pl.DeviceIdType.MESH,
        )

    def own_copy(b):
        return pltpu.make_async_copy(
            outgoing.at[b, me],
            back.at[me, :, pl.ds(b * 2 * BLOCK, 2 * BLOCK), :],
            own.at[b],
        )

    for b in range(blocks):
        count = min(BLOCK, share - b * BLOCK)
        if count < BLOCK:
            result[...] = jnp.zeros_like(result)

        def wave_step(r, carry):
            wave = owner[me * share + b * BLOCK + r]
            expanded = jnp.dot(
                pick[...].astype(BF16), legendre[b * BLOCK + r], preferred_element_type=F32
            ).astype(BF16)
            pieces = []
            for t in range(2):
                for h in range(halves):
                    start = b * 2 * BLOCK + t * BLOCK + r
                    piece = gathered[h, pl.ds(start, everything, stride=height), :]
                    pieces.append((piece * quad_slot[...]).astype(BF16))
            weighted = jnp.concatenate(pieces, axis=1)
            coefficient = lax.dot_general(
                expanded, weighted, (((0,), (0,)), ((), ())), preferred_element_type=F32
            )
            kept = degree >= wave
            factor = jnp.where(wave > 0, 2.0, 1.0).astype(F32)
            mixed = []
            for t in range(2):
                part = coefficient[:, t * channels : (t + 1) * channels] * gain[...]
                part = jnp.where(kept, part, 0.0).astype(BF16)
                mixed.append(jnp.dot(part, mix[...], preferred_element_type=F32).astype(BF16))
            synthesis = jnp.dot(
                expanded, jnp.concatenate(mixed, axis=1), preferred_element_type=F32
            ) * factor
            for t in range(2):
                for h in range(halves):
                    begin = t * channels + h * 128
                    result[h, pl.ds(t * BLOCK + r, everything, stride=2 * BLOCK), :] = synthesis[
                        :, begin : begin + 128
                    ]
            return carry

        lax.fori_loop(0, count, wave_step, 0)

        def narrow(i, carry):
            for s in range(slots):
                begin = pl.multiple_of((i * slots + s) * 2 * BLOCK, 8)
                outgoing[b, i, s] = jnp.concatenate(
                    [result[h, pl.ds(begin, 2 * BLOCK), :] for h in range(halves)], axis=1
                ).astype(BF16)
            return carry

        lax.fori_loop(0, n, narrow, 0)
        if b == 0:
            pl.semaphore_wait(barrier, n - 1)

        def start_block(i, carry):
            block_copy(i, b).start()
            return carry

        lax.fori_loop(1, n, start_block, 0)
        own_copy(b).start()

    for b in range(blocks):

        def wait_block(i, carry):
            block_copy(i, b).wait()
            return carry

        lax.fori_loop(1, n, wait_block, 0)
        own_copy(b).wait()


def inverse_kernel(back, table, out):
    block = back[...].reshape(table.shape[1], back.shape[2])
    out[0] = jnp.dot(table[...], block, preferred_element_type=F32).astype(BF16)


def body(
    n, grid_values, lat_counts, owner_wavenumber, legendre, quad_weight, spectral_gain, channel_mix
):
    slots, longitudes, channels = grid_values.shape
    waves = owner_wavenumber.shape[0]
    share, live_total, degrees = legendre.shape
    blocks = -(-share // BLOCK)
    padded = blocks * BLOCK
    height = 2 * padded
    everything = n * slots
    base = jnp.asarray(trig_table(waves, longitudes))
    slot_waves = owner_wavenumber.reshape(n, share)
    slot_waves = jnp.pad(slot_waves, ((0, 0), (0, padded - share)), constant_values=-2 * waves)
    slot_waves = slot_waves.reshape(n, blocks, 1, BLOCK)
    rows = jnp.concatenate([slot_waves, slot_waves + waves], axis=2).reshape(n * height, 1)

    vmem = pl.BlockSpec(memory_space=pltpu.VMEM)
    smem = pl.BlockSpec(memory_space=pltpu.SMEM)
    anywhere = pl.BlockSpec(memory_space=pl.ANY)
    limit = 60 * 1024 * 1024
    recv, back_table = pl.pallas_call(
        functools.partial(forward_kernel, "lat", n, live_total * longitudes),
        out_shape=(
            jax.ShapeDtypeStruct((n, slots, height, channels), BF16),
            jax.ShapeDtypeStruct((longitudes, n * height), BF16),
        ),
        in_specs=[smem, vmem, vmem, vmem],
        out_specs=(anywhere, vmem),
        scratch_shapes=[
            pltpu.VMEM((n, 2, channels), F32),
            pltpu.VMEM((n * height, longitudes), BF16),
            pltpu.VMEM((longitudes, channels), BF16),
            pltpu.VMEM((n, slots, height, channels), BF16),
            pltpu.SemaphoreType.DMA((n,)),
            pltpu.SemaphoreType.DMA((n,)),
            pltpu.SemaphoreType.DMA((n,)),
            pltpu.SemaphoreType.DMA((n,)),
            pltpu.SemaphoreType.DMA,
        ],
        compiler_params=pltpu.CompilerParams(
            collective_id=0, has_side_effects=True, vmem_limit_bytes=limit
        ),
    )(lat_counts, grid_values, base, rows)

    back = pl.pallas_call(
        functools.partial(middle_kernel, "lat", n, share),
        out_shape=jax.ShapeDtypeStruct((n, slots, height, channels), BF16),
        in_specs=[smem, smem, vmem, vmem, vmem, vmem, vmem],
        out_specs=anywhere,
        scratch_shapes=[
            pltpu.VMEM((channels // 128, everything * height, 128), F32),
            pltpu.VMEM((everything, live_total), F32),
            pltpu.VMEM((everything, 128), F32),
            pltpu.VMEM((blocks, n, slots, 2 * BLOCK, channels), BF16),
            pltpu.VMEM((channels // 128, everything * 2 * BLOCK, 128), F32),
            pltpu.SemaphoreType.DMA((blocks, n)),
            pltpu.SemaphoreType.DMA((blocks, n)),
            pltpu.SemaphoreType.DMA((blocks,)),
        ],
        compiler_params=pltpu.CompilerParams(
            collective_id=1, has_side_effects=True, vmem_limit_bytes=limit
        ),
    )(
        lat_counts, owner_wavenumber, recv, legendre, quad_weight.reshape(1, live_total),
        spectral_gain, channel_mix,
    )

    return pl.pallas_call(
        inverse_kernel,
        grid=(slots,),
        out_shape=jax.ShapeDtypeStruct((slots, longitudes, channels), BF16),
        in_specs=[
            pl.BlockSpec((n, None, height, channels), lambda s: (0, s, 0, 0)),
            pl.BlockSpec((longitudes, n * height), lambda s: (0, 0)),
        ],
        out_specs=pl.BlockSpec((1, longitudes, channels), lambda s: (s, 0, 0)),
        compiler_params=pltpu.CompilerParams(vmem_limit_bytes=limit),
    )(back, back_table)


def solution(mesh):
    return jax.shard_map(
        functools.partial(body, mesh.shape["lat"]),
        mesh=mesh,
        in_specs=(P(("group", "lat"), None, None), P(), P(), P("lat", None, None), P(), P(), P()),
        out_specs=P(("group", "lat"), None, None),
        check_vma=False,
    )
```

time: 340 us -> 157 us (0.46)
  Pallas kernels: 0 us -> 154 us
  local copies, waits for them, and re-layouts: 119 us -> 1.74 us
  waiting for transfers between devices: 109 us -> 0 us
  matrix products: 39.9 us -> 0 us
  other arithmetic: 25.5 us -> 0.03 us
  blocking collectives: 21.9 us -> 0 us
  starting transfers between devices: 21.5 us -> 0 us
    pallas_call x0 -> x3, Pallas kernels: none -> 154 us  [the longest x1 74.4 us: body(): pl.pallas_call(functools.partial(forward_kernel, 'lat', n, live_total * l...]
    all_to_all x2 -> x0, waiting for transfers between devices: 109 us -> none  [the longest x1 60.3 us: body(): lax.all_to_all(spectra, 'lat', split_axis=1, concat_axis=0, tiled=True)]
    reshape x5 -> x2, local copies, waits for them, and re-layouts: 47.7 us -> 1.7 us  [the longest x1 0.93 us: body(): jnp.concatenate([slot_waves, slot_waves + waves], axis=2)]
    dot_general x5 -> x0, matrix products: 39.9 us -> none  [the longest x1 9.92 us: body(): jnp.dot(filtered.reshape(-1, channels), channel_mix, preferred_element_ty...]
    convert_element_type x4 -> x0, local copies, waits for them, and re-layouts: 38.4 us -> none  [the longest x1 23.6 us: body(): filtered = (coefficient * degree_mask[:, :, None, None] * spectral_gain[N...]
    psum x1 -> x0, blocking collectives: 21.9 us -> none  [body(): lax.psum((jnp.sum(widened, axis=(0, 1)), jnp.sum(widened * widened, axis=...]
    all_to_all x2 -> x0, starting transfers between devices: 21.5 us -> none  [the longest x1 16.8 us: body(): lax.all_to_all(spectra, 'lat', split_axis=1, concat_axis=0, tiled=True)]
    another operation x3 -> x0, local copies, waits for them, and re-layouts: 14.5 us -> none  [the longest x1 6.89 us: inverse_table(): jnp.stack([jnp.cos(angle) * doubled, -jnp.sin(angle) * doubled], axis=1)]
  transfers between devices with their start and end apart: 2 -> 0, of which waited for: 2 -> 0; matrix products, arithmetic and copies ran while one was open for 4% -> 0% of each run, Pallas kernels for 0% -> 0%
where the time goes in v1:
time: 157 us; the launch traced here: 156 us
  Pallas kernels  154 us (98%)
  local copies, waits for them, and re-layouts  1.74 us (1%)
    pallas_call x1, Pallas kernels, body(): pl.pallas_call(functools.partial(forward_kernel, 'lat', n, live_total * l...  74.4 us
    pallas_call x1, Pallas kernels, body(): pl.pallas_call(functools.partial(middle_kernel, 'lat', n, share), out_sha...  70 us
    pallas_call x1, Pallas kernels, body(): pl.pallas_call(inverse_kernel, grid=(slots,), out_shape=jax.ShapeDtypeStr...  9.5 us

profile of v1, /device:TPU:13, one launch (start us, length us, event | category | flops | bytes accessed | tf_op | source)
XLA Modules:
  0.0 155.7 jit_solution(9871382457232112751)
XLA Ops:
  0.0 0.8 reshape.23
  0.9 0.9 reshape.26.rows
  1.8 74.4 %shard_map.82 = (bf16[16,7,48,256]{3,2,1,0:T(8,128)(2,1)}, bf16[1440,768]{1,0:T(8,128)(2,1)}) custom-call(s32[16]{0:T(128)} %counts.3, bf16[7,1440,256]{2,1,0:T(8,128)(2,1)} %x.1, bf16[768,1440]{1,0:T(8,128)(2,1)} %constant.1.clone.base, s32[768,1]{1,0:T(8,128)} %reshape.26.rows), custom_call_target="tpu_custom_call" | custom-call | tf_op jit(solution)/shard_map/pallas_call | solution.py:277
  76.3 70.0 %shard_map.83.back = bf16[16,7,48,256]{3,2,1,0:T(8,128)(2,1)} custom-call(s32[16]{0:T(128)} %counts.3, s32[384]{0:T(512)} %owner.1, bf16[16,7,48,256]{3,2,1,0:T(8,128)(2,1)} %get-tuple-element.7.spectra, bf16[24,96,384]{2,1,0:T(8,128)(2,1)} %legendre.1, f32[1,96]{1,0:T(1,128)} %bitcast.1, f32[384,256]{1,0:T(8,128)} %gain.1, bf16[256,256]{1,0:T(8,128)(2,1)} %mix.1), custom_call_target="tpu_custom_call" | custom-call | tf_op jit(solution)/shard_map/pallas_call | solution.py:301
  146.2 9.5 %shard_map.84 = bf16[7,1440,256]{2,1,0:T(8,128)(2,1)} custom-call(bf16[16,7,48,256]{3,2,1,0:T(8,128)(2,1)} %shard_map.83.back, bf16[1440,768]{1,0:T(8,128)(2,1)} %get-tuple-element.8.table), custom_call_target="tpu_custom_call" | custom-call | tf_op jit(solution)/shard_map/pallas_call | solution.py:324
  (3 shorter events, 0.1 us)

commit v2 on v1

v2 whole, which is shorter than its diff:
```python
import functools
import math

import jax
import jax.numpy as jnp
import numpy as np
from jax import lax
from jax.experimental import pallas as pl
from jax.experimental.pallas import tpu as pltpu
from jax.sharding import PartitionSpec as P

BLOCK = 8
F32 = jnp.float32
BF16 = jnp.bfloat16


def trig_table(waves, longitudes):
    phase = np.arange(waves)[:, None] * np.arange(longitudes)[None, :] % longitudes
    angle = phase * (2.0 * math.pi / longitudes)
    factor = 1.0 / math.sqrt(longitudes)
    table = np.concatenate([np.cos(angle) * factor, -np.sin(angle) * factor], axis=0)
    return table.astype(BF16)


def greet_all(axis, count, me):
    barrier = pltpu.get_barrier_semaphore()

    def signal(i, carry):
        other = lax.rem(me + i, count)
        pl.semaphore_signal(
            barrier, inc=1, device_id={axis: other}, device_id_type=pl.DeviceIdType.MESH
        )
        return carry

    lax.fori_loop(1, count, signal, 0)
    return barrier


def spectral_kernel(
    axis, n, points, share, counts, owner, x, base, rows, legendre, quad, gain, mix,
    back, back_table,
    sums, table, normed, spec, recv, gathered, pick, quad_slot, outgoing, result,
    mom_send, mom_recv, send, arrive, own, back_send, back_arrive, back_own,
):
    me = lax.axis_index(axis)
    slots, channels = x.shape[0], x.shape[2]
    everything = n * slots
    live_total, degrees = legendre.shape[1], legendre.shape[2]
    halves = channels // 128
    blocks = spec.shape[0]
    lines = n * 2 * BLOCK
    barrier = greet_all(axis, n, me)
    live = counts[me]
    zero = jnp.zeros((1, channels), F32)

    def add_slot(s, carry):
        first, second = carry
        wide = x[s].astype(F32)
        weight = jnp.where(s < live, 1.0, 0.0).astype(F32)
        first = first + weight * jnp.sum(wide, axis=0, keepdims=True)
        second = second + weight * jnp.sum(wide * wide, axis=0, keepdims=True)
        return first, second

    first, second = lax.fori_loop(0, slots, add_slot, (zero, zero))
    sums[me, 0:1, :] = first
    sums[me, 1:2, :] = second
    pl.semaphore_wait(barrier, n - 1)

    def moment_copy(i):
        other = lax.rem(me + i, n)
        return pltpu.make_async_remote_copy(
            src_ref=sums.at[me], dst_ref=sums.at[me],
            send_sem=mom_send.at[i], recv_sem=mom_recv.at[i],
            device_id={axis: other}, device_id_type=pl.DeviceIdType.MESH,
        )

    def start_moment(i, carry):
        moment_copy(i).start()
        return carry

    def wait_moment(i, carry):
        moment_copy(i).wait()
        return carry

    lax.fori_loop(1, n, start_moment, 0)
    total = base.shape[0]
    chosen = rows[...] == lax.broadcasted_iota(jnp.int32, (rows.shape[0], total), 1)
    chosen = jnp.where(chosen, 1.0, 0.0).astype(BF16)
    table[...] = jnp.dot(chosen, base[...], preferred_element_type=F32).astype(BF16)
    lax.fori_loop(1, n, wait_moment, 0)
    both = jnp.sum(sums[...], axis=0)
    mean = both[0:1] / points
    variance = both[1:2] / points - mean * mean
    scale = lax.rsqrt(variance + 1e-05)

    def block_copy(b, i):
        other = lax.rem(me + i, n)
        return pltpu.make_async_remote_copy(
            src_ref=spec.at[b, other], dst_ref=recv.at[b, me],
            send_sem=send.at[b, i], recv_sem=arrive.at[b, i],
            device_id={axis: other}, device_id_type=pl.DeviceIdType.MESH,
        )

    for b in range(blocks):

        def slot_step(s, carry):
            if b == 0:
                weight = jnp.where(s < live, 1.0, 0.0).astype(F32)
                normed[s] = ((x[s].astype(F32) - mean) * scale * weight).astype(BF16)
            out = jnp.dot(
                table[b * lines : (b + 1) * lines], normed[s], preferred_element_type=F32
            )
            spec[b, :, s] = out.astype(BF16).reshape(n, 2 * BLOCK, channels)
            if b == 0:

                def start_slot(i, inner):
                    other = lax.rem(me + i, n)
                    pltpu.make_async_remote_copy(
                        src_ref=spec.at[b, other, s], dst_ref=recv.at[b, me, s],
                        send_sem=send.at[b, i], recv_sem=arrive.at[b, i],
                        device_id={axis: other}, device_id_type=pl.DeviceIdType.MESH,
                    ).start()
                    return inner

                lax.fori_loop(1, n, start_slot, 0)
            return carry

        lax.fori_loop(0, slots, slot_step, 0)
        if b > 0:

            def start_block(i, carry):
                block_copy(b, i).start()
                return carry

            lax.fori_loop(1, n, start_block, 0)
        pltpu.make_async_copy(spec.at[b, me], recv.at[b, me], own.at[b]).start()

    back_table[...] = table[...].T
    row = lax.broadcasted_iota(jnp.int32, (everything, live_total), 0)
    lane = lax.broadcasted_iota(jnp.int32, (everything, live_total), 1)
    pick[...] = jnp.zeros_like(pick)

    def mark(i, begin):
        within = row - i * slots
        hit = (within >= 0) & (within < counts[i]) & (lane == begin + within)
        pick[...] += jnp.where(hit, 1.0, 0.0).astype(F32)
        return begin + counts[i]

    lax.fori_loop(0, n, mark, jnp.int32(0))
    quad_slot[...] = jnp.broadcast_to(
        jnp.sum(pick[...] * quad[...], axis=1, keepdims=True), quad_slot.shape
    )
    degree = lax.broadcasted_iota(jnp.int32, (degrees, channels), 0)

    def return_copy(b, i):
        other = lax.rem(me + i, n)
        return pltpu.make_async_remote_copy(
            src_ref=outgoing.at[b, other], dst_ref=back.at[b, me],
            send_sem=back_send.at[b, i], recv_sem=back_arrive.at[b, i],
            device_id={axis: other}, device_id_type=pl.DeviceIdType.MESH,
        )

    for b in range(blocks):
        count = min(BLOCK, share - b * BLOCK)
        if count < BLOCK:
            result[...] = jnp.zeros_like(result)

        def wait_block(i, carry):
            block_copy(b, i).wait()
            return carry

        lax.fori_loop(1, n, wait_block, 0)
        pltpu.make_async_copy(spec.at[b, me], recv.at[b, me], own.at[b]).wait()

        def widen(i, carry):
            for s in range(slots):
                wide = recv[b, i, s].astype(F32)
                begin = pl.multiple_of((i * slots + s) * 2 * BLOCK, 8)
                for h in range(halves):
                    gathered[h, pl.ds(begin, 2 * BLOCK), :] = wide[:, h * 128 : (h + 1) * 128]
            return carry

        lax.fori_loop(0, n, widen, 0)

        def wave_step(r, carry):
            wave = owner[me * share + b * BLOCK + r]
            expanded = jnp.dot(
                pick[...].astype(BF16), legendre[b * BLOCK + r], preferred_element_type=F32
            ).astype(BF16)
            pieces = []
            for t in range(2):
                for h in range(halves):
                    piece = gathered[h, pl.ds(t * BLOCK + r, everything, stride=2 * BLOCK), :]
                    pieces.append((piece * quad_slot[...]).astype(BF16))
            weighted = jnp.concatenate(pieces, axis=1)
            coefficient = lax.dot_general(
                expanded, weighted, (((0,), (0,)), ((), ())), preferred_element_type=F32
            )
            kept = degree >= wave
            factor = jnp.where(wave > 0, 2.0, 1.0).astype(F32)
            mixed = []
            for t in range(2):
                part = coefficient[:, t * channels : (t + 1) * channels] * gain[...]
                part = jnp.where(kept, part, 0.0).astype(BF16)
                mixed.append(jnp.dot(part, mix[...], preferred_element_type=F32).astype(BF16))
            synthesis = jnp.dot(
                expanded, jnp.concatenate(mixed, axis=1), preferred_element_type=F32
            ) * factor
            for t in range(2):
                for h in range(halves):
                    begin = t * channels + h * 128
                    result[h, pl.ds(t * BLOCK + r, everything, stride=2 * BLOCK), :] = synthesis[
                        :, begin : begin + 128
                    ]
            return carry

        lax.fori_loop(0, count, wave_step, 0)

        def narrow(i, carry):
            for s in range(slots):
                begin = pl.multiple_of((i * slots + s) * 2 * BLOCK, 8)
                outgoing[b, i, s] = jnp.concatenate(
                    [result[h, pl.ds(begin, 2 * BLOCK), :] for h in range(halves)], axis=1
                ).astype(BF16)
            return carry

        lax.fori_loop(0, n, narrow, 0)

        def start_return(i, carry):
            return_copy(b, i).start()
            return carry

        lax.fori_loop(1, n, start_return, 0)
        pltpu.make_async_copy(outgoing.at[b, me], back.at[b, me], back_own.at[b]).start()

    for b in range(blocks):

        def wait_return(i, carry):
            return_copy(b, i).wait()
            return carry

        lax.fori_loop(1, n, wait_return, 0)
        pltpu.make_async_copy(outgoing.at[b, me], back.at[b, me], back_own.at[b]).wait()


def inverse_kernel(back, table, out):
    block = back[...].reshape(table.shape[1], back.shape[-1])
    out[0] = jnp.dot(table[...], block, preferred_element_type=F32).astype(BF16)


def body(
    n, grid_values, lat_counts, owner_wavenumber, legendre, quad_weight, spectral_gain, channel_mix
):
    slots, longitudes, channels = grid_values.shape
    waves = owner_wavenumber.shape[0]
    share, live_total, degrees = legendre.shape
    blocks = -(-share // BLOCK)
    padded = blocks * BLOCK
    everything = n * slots
    base = jnp.asarray(trig_table(waves, longitudes))
    slot_waves = owner_wavenumber.reshape(n, share)
    slot_waves = jnp.pad(slot_waves, ((0, 0), (0, padded - share)), constant_values=-2 * waves)
    slot_waves = slot_waves.reshape(n, blocks, 1, BLOCK).transpose(1, 0, 2, 3)
    rows = jnp.concatenate([slot_waves, slot_waves + waves], axis=2).reshape(-1, 1)

    vmem = pl.BlockSpec(memory_space=pltpu.VMEM)
    smem = pl.BlockSpec(memory_space=pltpu.SMEM)
    anywhere = pl.BlockSpec(memory_space=pl.ANY)
    limit = 60 * 1024 * 1024
    packet = (blocks, n, slots, 2 * BLOCK, channels)
    copies = pltpu.SemaphoreType.DMA
    back, back_table = pl.pallas_call(
        functools.partial(spectral_kernel, "lat", n, live_total * longitudes, share),
        out_shape=(
            jax.ShapeDtypeStruct(packet, BF16),
            jax.ShapeDtypeStruct((longitudes, blocks * n * 2 * BLOCK), BF16),
        ),
        in_specs=[smem, smem] + [vmem] * 7,
        out_specs=(anywhere, vmem),
        scratch_shapes=[
            pltpu.VMEM((n, 2, channels), F32),
            pltpu.VMEM((blocks * n * 2 * BLOCK, longitudes), BF16),
            pltpu.VMEM((slots, longitudes, channels), BF16),
            pltpu.VMEM(packet, BF16),
            pltpu.VMEM(packet, BF16),
            pltpu.VMEM((channels // 128, everything * 2 * BLOCK, 128), F32),
            pltpu.VMEM((everything, live_total), F32),
            pltpu.VMEM((everything, 128), F32),
            pltpu.VMEM(packet, BF16),
            pltpu.VMEM((channels // 128, everything * 2 * BLOCK, 128), F32),
            copies((n,)), copies((n,)),
            copies((blocks, n)), copies((blocks, n)), copies((blocks,)),
            copies((blocks, n)), copies((blocks, n)), copies((blocks,)),
        ],
        compiler_params=pltpu.CompilerParams(
            collective_id=0, has_side_effects=True, vmem_limit_bytes=limit
        ),
    )(
        lat_counts, owner_wavenumber, grid_values, base, rows, legendre,
        quad_weight.reshape(1, live_total), spectral_gain, channel_mix,
    )

    return pl.pallas_call(
        inverse_kernel,
        grid=(slots,),
        out_shape=jax.ShapeDtypeStruct((slots, longitudes, channels), BF16),
        in_specs=[
            pl.BlockSpec((blocks, n, None, 2 * BLOCK, channels), lambda s: (0, 0, s, 0, 0)),
            pl.BlockSpec((longitudes, blocks * n * 2 * BLOCK), lambda s: (0, 0)),
        ],
        out_specs=pl.BlockSpec((1, longitudes, channels), lambda s: (s, 0, 0)),
        compiler_params=pltpu.CompilerParams(vmem_limit_bytes=limit),
    )(back, back_table)


def solution(mesh):
    return jax.shard_map(
        functools.partial(body, mesh.shape["lat"]),
        mesh=mesh,
        in_specs=(P(("group", "lat"), None, None), P(), P(), P("lat", None, None), P(), P(), P()),
        out_specs=P(("group", "lat"), None, None),
        check_vma=False,
    )
```

time: 157 us -> 148 us (0.943)
  Pallas kernels: 154 us -> 145 us
    pallas_call x2 -> x1, Pallas kernels: 144 us -> 136 us  [body(): pl.pallas_call(functools.partial(spectral_kernel, 'lat', n, live_total *...]
where the time goes in v2:
time: 148 us; the launch traced here: 147 us
  Pallas kernels  145 us (98%)
  local copies, waits for them, and re-layouts  1.74 us (1%)
    pallas_call x1, Pallas kernels, body(): pl.pallas_call(functools.partial(spectral_kernel, 'lat', n, live_total *...  136 us
    pallas_call x1, Pallas kernels, body(): pl.pallas_call(inverse_kernel, grid=(slots,), out_shape=jax.ShapeDtypeStr...  9.51 us

profile of v2, /device:TPU:13, one launch (start us, length us, event | category | flops | bytes accessed | tf_op | source)
XLA Modules:
  0.0 147.3 jit_solution(10686739035035716067)
XLA Ops:
  0.0 0.8 reshape.11
  0.9 0.9 reshape.14.rows
  1.8 135.9 %shard_map.82 = (bf16[3,16,7,16,256]{4,3,2,1,0:T(8,128)(2,1)}, bf16[1440,768]{1,0:T(8,128)(2,1)}) custom-call(s32[16]{0:T(128)} %counts.1, s32[384]{0:T(512)} %owner.1, bf16[7,1440,256]{2,1,0:T(8,128)(2,1)} %x.1, bf16[768,1440]{1,0:T(8,128)(2,1)} %constant.1.clone.base, s32[768,1]{1,0:T(8,128)} %reshape.14.rows, bf16[24,96,384]{2,1,0:T(8,128)(2,1)} %legendre.1, ...), custom_call_target="tpu_custom_call" | custom-call | tf_op jit(solution)/shard_map/pallas_call | solution.py:272
  137.7 9.5 %shard_map.83 = bf16[7,1440,256]{2,1,0:T(8,128)(2,1)} custom-call(bf16[3,16,7,16,256]{4,3,2,1,0:T(8,128)(2,1)} %get-tuple-element.7.back, bf16[1440,768]{1,0:T(8,128)(2,1)} %get-tuple-element.8.table), custom_call_target="tpu_custom_call" | custom-call | tf_op jit(solution)/shard_map/pallas_call | solution.py:303
  (3 shorter events, 0.1 us)

commit v3 on v2

--- a/solution.py
+++ b/solution.py
@@ -37,10 +37,11 @@
 
 
 def spectral_kernel(
-    axis, n, points, share, counts, owner, x, base, rows, legendre, quad, gain, mix,
-    back, back_table,
-    sums, table, normed, spec, recv, gathered, pick, quad_slot, outgoing, result,
-    mom_send, mom_recv, send, arrive, own, back_send, back_arrive, back_own,
+    axis, n, points, share, counts, owner, x, base_far, waves_lane, legendre_far, quad, gain_far,
+    mix, last, back_table, partial,
+    sums, full, table, front, normed, spec, recv, gathered, pick, quad_slot, outgoing, result,
+    early, base, legendre, gain,
+    load, fetch, mom_send, mom_recv, send, arrive, own, back_send, back_arrive, back_own, store,
 ):
     me = lax.axis_index(axis)
     slots, channels = x.shape[0], x.shape[2]
@@ -49,21 +50,39 @@
     halves = channels // 128
     blocks = spec.shape[0]
     lines = n * 2 * BLOCK
+    padded = blocks * BLOCK
+
+    def load_slot(s):
+        return pltpu.make_async_copy(x.at[s], normed.at[s], load.at[s])
+
+    def start_load(s, carry):
+        load_slot(s).start()
+        return carry
+
+    lax.fori_loop(0, slots, start_load, 0)
+    base_copy = pltpu.make_async_copy(base_far, base, fetch.at[0])
+    legendre_copy = pltpu.make_async_copy(legendre_far, legendre, fetch.at[1])
+    gain_copy = pltpu.make_async_copy(gain_far, gain, fetch.at[2])
+    base_copy.start()
+    legendre_copy.start()
+    gain_copy.start()
     barrier = greet_all(axis, n, me)
     live = counts[me]
-    zero = jnp.zeros((1, channels), F32)
+    group = math.gcd(x.shape[1], 32)
+    zero = jnp.zeros((group, channels), F32)
 
     def add_slot(s, carry):
         first, second = carry
-        wide = x[s].astype(F32)
+        load_slot(s).wait()
+        wide = normed[s].astype(F32).reshape(-1, group, channels)
         weight = jnp.where(s < live, 1.0, 0.0).astype(F32)
-        first = first + weight * jnp.sum(wide, axis=0, keepdims=True)
-        second = second + weight * jnp.sum(wide * wide, axis=0, keepdims=True)
+        first = first + weight * jnp.sum(wide, axis=0)
+        second = second + weight * jnp.sum(wide * wide, axis=0)
         return first, second
 
     first, second = lax.fori_loop(0, slots, add_slot, (zero, zero))
-    sums[me, 0:1, :] = first
-    sums[me, 1:2, :] = second
+    sums[me, 0:1, :] = jnp.sum(first, axis=0, keepdims=True)
+    sums[me, 1:2, :] = jnp.sum(second, axis=0, keepdims=True)
     pl.semaphore_wait(barrier, n - 1)
 
     def moment_copy(i):
@@ -83,10 +102,25 @@
         return carry
 
     lax.fori_loop(1, n, start_moment, 0)
-    total = base.shape[0]
-    chosen = rows[...] == lax.broadcasted_iota(jnp.int32, (rows.shape[0], total), 1)
-    chosen = jnp.where(chosen, 1.0, 0.0).astype(BF16)
-    table[...] = jnp.dot(chosen, base[...], preferred_element_type=F32).astype(BF16)
+    waves = base.shape[0] // 2
+    natural = lax.broadcasted_iota(jnp.int32, (waves, n * padded), 0)
+    chosen = jnp.where(natural == waves_lane[...], 1.0, 0.0).astype(BF16)
+    base_copy.wait()
+    for t in range(2):
+        full[t] = lax.dot_general(
+            chosen, base[t * waves : (t + 1) * waves], (((0,), (0,)), ((), ())),
+            preferred_element_type=F32,
+        )
+
+    def order_rows(o, carry):
+        for b in range(blocks):
+            begin = pl.multiple_of(o * padded + b * BLOCK, BLOCK)
+            both = [full[t, pl.ds(begin, BLOCK), :] for t in range(2)]
+            begin = pl.multiple_of((b * n + o) * 2 * BLOCK, 2 * BLOCK)
+            table[pl.ds(begin, 2 * BLOCK), :] = jnp.concatenate(both, axis=0).astype(BF16)
+        return carry
+
+    lax.fori_loop(0, n, order_rows, 0)
     lax.fori_loop(1, n, wait_moment, 0)
     both = jnp.sum(sums[...], axis=0)
     mean = both[0:1] / points
@@ -106,7 +140,7 @@
         def slot_step(s, carry):
             if b == 0:
                 weight = jnp.where(s < live, 1.0, 0.0).astype(F32)
-                normed[s] = ((x[s].astype(F32) - mean) * scale * weight).astype(BF16)
+                normed[s] = ((normed[s].astype(F32) - mean) * scale * weight).astype(BF16)
             out = jnp.dot(
                 table[b * lines : (b + 1) * lines], normed[s], preferred_element_type=F32
             )
@@ -135,7 +169,12 @@
             lax.fori_loop(1, n, start_block, 0)
         pltpu.make_async_copy(spec.at[b, me], recv.at[b, me], own.at[b]).start()
 
-    back_table[...] = table[...].T
+    late = (blocks - 1) * lines
+    back_table[...] = table[late:].T
+    if blocks > 1:
+        front[...] = table[:late].T
+    legendre_copy.wait()
+    gain_copy.wait()
     row = lax.broadcasted_iota(jnp.int32, (everything, live_total), 0)
     lane = lax.broadcasted_iota(jnp.int32, (everything, live_total), 1)
     pick[...] = jnp.zeros_like(pick)
@@ -152,10 +191,13 @@
     )
     degree = lax.broadcasted_iota(jnp.int32, (degrees, channels), 0)
 
+    def landing(b):
+        return early.at[b, me] if b < blocks - 1 else last.at[me]
+
     def return_copy(b, i):
         other = lax.rem(me + i, n)
         return pltpu.make_async_remote_copy(
-            src_ref=outgoing.at[b, other], dst_ref=back.at[b, me],
+            src_ref=outgoing.at[b, other], dst_ref=landing(b),
             send_sem=back_send.at[b, i], recv_sem=back_arrive.at[b, i],
             device_id={axis: other}, device_id_type=pl.DeviceIdType.MESH,
         )
@@ -231,21 +273,44 @@
             return carry
 
         lax.fori_loop(1, n, start_return, 0)
-        pltpu.make_async_copy(outgoing.at[b, me], back.at[b, me], back_own.at[b]).start()
-
-    for b in range(blocks):
-
+        pltpu.make_async_copy(outgoing.at[b, me], landing(b), back_own.at[b]).start()
+
+    def settle(b):
         def wait_return(i, carry):
             return_copy(b, i).wait()
             return carry
 
         lax.fori_loop(1, n, wait_return, 0)
-        pltpu.make_async_copy(outgoing.at[b, me], back.at[b, me], back_own.at[b]).wait()
-
-
-def inverse_kernel(back, table, out):
-    block = back[...].reshape(table.shape[1], back.shape[-1])
-    out[0] = jnp.dot(table[...], block, preferred_element_type=F32).astype(BF16)
+        pltpu.make_async_copy(outgoing.at[b, me], landing(b), back_own.at[b]).wait()
+
+    def store_slot(s):
+        return pltpu.make_async_copy(normed.at[s], partial.at[s], store.at[s])
+
+    for b in range(blocks - 1):
+        settle(b)
+
+    def partial_slot(s, carry):
+        if blocks > 1:
+            block = early[:, :, s].reshape(late, channels)
+            normed[s] = jnp.dot(front[...], block, preferred_element_type=F32).astype(BF16)
+        else:
+            normed[s] = jnp.zeros(normed.shape[1:], BF16)
+        store_slot(s).start()
+        return carry
+
+    def wait_store(s, carry):
+        store_slot(s).wait()
+        return carry
+
+    lax.fori_loop(0, slots, partial_slot, 0)
+    lax.fori_loop(0, slots, wait_store, 0)
+    settle(blocks - 1)
+
+
+def inverse_kernel(last, table, partial, out):
+    block = last[...].reshape(table.shape[1], last.shape[-1])
+    total = jnp.dot(table[...], block, preferred_element_type=F32)
+    out[0] = (partial[0].astype(F32) + total).astype(BF16)
 
 
 def body(
@@ -259,9 +324,8 @@
     everything = n * slots
     base = jnp.asarray(trig_table(waves, longitudes))
     slot_waves = owner_wavenumber.reshape(n, share)
-    slot_waves = jnp.pad(slot_waves, ((0, 0), (0, padded - share)), constant_values=-2 * waves)
-    slot_waves = slot_waves.reshape(n, blocks, 1, BLOCK).transpose(1, 0, 2, 3)
-    rows = jnp.concatenate([slot_waves, slot_waves + waves], axis=2).reshape(-1, 1)
+    slot_waves = jnp.pad(slot_waves, ((0, 0), (0, padded - share)), constant_values=-1)
+    waves_lane = slot_waves.reshape(1, n * padded)
 
     vmem = pl.BlockSpec(memory_space=pltpu.VMEM)
     smem = pl.BlockSpec(memory_space=pltpu.SMEM)
@@ -269,17 +333,21 @@
     limit = 60 * 1024 * 1024
     packet = (blocks, n, slots, 2 * BLOCK, channels)
     copies = pltpu.SemaphoreType.DMA
-    back, back_table = pl.pallas_call(
+    lines = n * 2 * BLOCK
+    last, back_table, partial = pl.pallas_call(
         functools.partial(spectral_kernel, "lat", n, live_total * longitudes, share),
         out_shape=(
-            jax.ShapeDtypeStruct(packet, BF16),
-            jax.ShapeDtypeStruct((longitudes, blocks * n * 2 * BLOCK), BF16),
+            jax.ShapeDtypeStruct(packet[1:], BF16),
+            jax.ShapeDtypeStruct((longitudes, lines), BF16),
+            jax.ShapeDtypeStruct((slots, longitudes, channels), BF16),
         ),
-        in_specs=[smem, smem] + [vmem] * 7,
-        out_specs=(anywhere, vmem),
+        in_specs=[smem, smem, anywhere, anywhere, vmem, anywhere, vmem, anywhere, vmem],
+        out_specs=(anywhere, vmem, anywhere),
         scratch_shapes=[
             pltpu.VMEM((n, 2, channels), F32),
-            pltpu.VMEM((blocks * n * 2 * BLOCK, longitudes), BF16),
+            pltpu.VMEM((2, n * padded, longitudes), F32),
+            pltpu.VMEM((blocks * lines, longitudes), BF16),
+            pltpu.VMEM((longitudes, max(blocks - 1, 1) * lines), BF16),
             pltpu.VMEM((slots, longitudes, channels), BF16),
             pltpu.VMEM(packet, BF16),
             pltpu.VMEM(packet, BF16),
@@ -288,15 +356,21 @@
             pltpu.VMEM((everything, 128), F32),
             pltpu.VMEM(packet, BF16),
             pltpu.VMEM((channels // 128, everything * 2 * BLOCK, 128), F32),
+            pltpu.VMEM((max(blocks - 1, 1),) + packet[1:], BF16),
+            pltpu.VMEM(base.shape, BF16),
+            pltpu.VMEM(legendre.shape, BF16),
+            pltpu.VMEM(spectral_gain.shape, F32),
+            copies((slots,)), copies((3,)),
             copies((n,)), copies((n,)),
             copies((blocks, n)), copies((blocks, n)), copies((blocks,)),
             copies((blocks, n)), copies((blocks, n)), copies((blocks,)),
+            copies((slots,)),
         ],
         compiler_params=pltpu.CompilerParams(
             collective_id=0, has_side_effects=True, vmem_limit_bytes=limit
         ),
     )(
-        lat_counts, owner_wavenumber, grid_values, base, rows, legendre,
+        lat_counts, owner_wavenumber, grid_values, base, waves_lane, legendre,
         quad_weight.reshape(1, live_total), spectral_gain, channel_mix,
     )
 
@@ -305,12 +379,13 @@
         grid=(slots,),
         out_shape=jax.ShapeDtypeStruct((slots, longitudes, channels), BF16),
         in_specs=[
-            pl.BlockSpec((blocks, n, None, 2 * BLOCK, channels), lambda s: (0, 0, s, 0, 0)),
-            pl.BlockSpec((longitudes, blocks * n * 2 * BLOCK), lambda s: (0, 0)),
+            pl.BlockSpec((n, None, 2 * BLOCK, channels), lambda s: (0, s, 0, 0)),
+            pl.BlockSpec((longitudes, lines), lambda s: (0, 0)),
+            pl.BlockSpec((1, longitudes, channels), lambda s: (s, 0, 0)),
         ],
         out_specs=pl.BlockSpec((1, longitudes, channels), lambda s: (s, 0, 0)),
         compiler_params=pltpu.CompilerParams(vmem_limit_bytes=limit),
-    )(back, back_table)
+    )(last, back_table, partial)
 
 
 def solution(mesh):

time: 148 us -> 143 us (0.966)
  Pallas kernels: 145 us -> 142 us
    pallas_call x1, Pallas kernels: 136 us -> 133 us  [body(): pl.pallas_call(functools.partial(spectral_kernel, 'lat', n, live_total *...]
where the time goes in v3:
time: 143 us
  Pallas kernels  142 us (99%)
    pallas_call x1, Pallas kernels, body(): pl.pallas_call(functools.partial(spectral_kernel, 'lat', n, live_total *...  133 us
    pallas_call x1, Pallas kernels, body(): pl.pallas_call(inverse_kernel, grid=(slots,), out_shape=jax.ShapeDtypeStr...  8.9 us

profile of v3, /device:TPU:13, one launch (start us, length us, event | category | flops | bytes accessed | tf_op | source)
XLA Modules:
  0.0 142.9 jit_solution(18325281875135338358)
XLA Ops:
  0.0 1.2 reshape.8.waves_lane
  1.2 132.7 %shard_map.82 = (bf16[16,7,16,256]{3,2,1,0:T(8,128)(2,1)}, bf16[1440,256]{1,0:T(8,128)(2,1)}, bf16[7,1440,256]{2,1,0:T(8,128)(2,1)}) custom-call(s32[16]{0:T(128)} %counts.1, s32[384]{0:T(512)} %owner.1, bf16[7,1440,256]{2,1,0:T(8,128)(2,1)} %x.1, bf16[768,1440]{1,0:T(8,128)(2,1)} %constant.1.clone.base_far, s32[1,384]{1,0:T(1,128)} %reshape.8.waves_lane, ...), custom_call_target="tpu_custom_call" | custom-call | tf_op jit(solution)/shard_map/pallas_call | solution.py:337
  134.0 8.9 %shard_map.83 = bf16[7,1440,256]{2,1,0:T(8,128)(2,1)} custom-call(bf16[16,7,16,256]{3,2,1,0:T(8,128)(2,1)} %get-tuple-element.8.last, bf16[1440,256]{1,0:T(8,128)(2,1)} %get-tuple-element.9.table, bf16[7,1440,256]{2,1,0:T(8,128)(2,1)} %get-tuple-element.10.partial), custom_call_target="tpu_custom_call" | custom-call | tf_op jit(solution)/shard_map/pallas_call | solution.py:377
